TPU v7x, 32 devices: a whole 2x2x4 slice. The times are simulated.
32 devices in a mesh: blk: 4 (over x, core), grp: 8 (over z, y).
Axes of the slice: x: 2, y: 2, z: 4, core: 2. Of those that a mesh axis runs over, the one named last changes fastest.
Arguments:
- features: float32 [49152, 256], P(('blk', 'grp')), may hold values from -6 to 6
- initial: bfloat16 [49152, 256], P(('blk', 'grp')), may hold values from -6 to 6
- history: bfloat16 [49152, 256], P(('blk', 'grp')), may hold values from -6 to 6
- weight: bfloat16 [256, 256], replicated, may hold values from -0.375 to 0.375
- column_ids: int32 [384, 16], P(('blk', 'grp')), may hold values from 0 to 23, as said below
- block_values: bfloat16 [384, 16, 128, 128], P(('blk', 'grp')), may hold values from -0.125 to 0.125
- group_table: int32 [4, 8, 8], P('blk'), may hold values from 0 to 11
- loop_table: int32 [8, 4, 4], P('grp'), may hold values from 0 to 11
Outputs:
- refreshed: float32 [49152, 256], P(('blk', 'grp'))
- inbox: float32 [49152, 256], P(('blk', 'grp'))
Inputs may be any that keep to these rules, and one draw needn't show every extreme that they name: `column_ids`: among the 16 entries of the 12 row tiles of one device, every slot from 0 to 12 + 8 + 4 - 1 appears at least once.
All inputs are finite; a program needn't handle non-finite values.
Results may differ from a plain program's by a relative error of at most 0.004.
Values may be sent and summed in bfloat16 or wider, within the bound.
A program may use at most 128 MiB of HBM per device.

v0:
```python
import functools

import jax
import jax.numpy as jnp
from jax import lax
from jax.experimental import pallas as pl
from jax.experimental.pallas import tpu as pltpu
from jax.sharding import PartitionSpec as P

teleport = 0.1
mapping_share = 0.5
MAIN_LIMIT = 44 * 1024 * 1024
DELIVER_LIMIT = 6 * 1024 * 1024
MESH = pl.DeviceIdType.MESH
GATHER_UNROLL = 12
REFRESH_UNROLL = 12
MESSAGE_UNROLL = 32


def partners(position, size, axis):
    found = []
    for step in range(size - 1, 0, -1):
        if size & (size - 1) == 0:
            there = position
            bit = 1
            while bit < size:
                if step & bit:
                    there = there + bit * (1 - 2 * lax.rem(lax.div(position, bit), 2))
                bit *= 2
            found.append((axis, there))
        else:
            found.append((axis, lax.rem(position + step, size)))
    return found


def slot_plan(ids_ref, plan, tiles, entries, remote, pairs):
    count = tiles * entries
    width = plan.shape[1]
    iota = lambda shape, axis: lax.broadcasted_iota(jnp.int32, shape, axis)
    total = lambda value, axis: jnp.sum(value, axis=axis, keepdims=True)
    lane = iota((1, count), 1)
    row = jnp.zeros((1, count), jnp.int32)
    for t in range(tiles):
        for k in range(entries):
            row = jnp.where(lane == t * entries + k, ids_ref[t, k] - tiles, row)
    down, across = iota((count, count), 0), iota((count, count), 1)
    column = total(jnp.where(down == across, row, 0), 1)
    even = lambda value: value + lax.rem(value, 2)
    sizes_row = even(total((column == iota((count, remote), 1)).astype(jnp.int32), 0))
    sizes_column = even(total((row == iota((remote, count), 0)).astype(jnp.int32), 1))
    low, high = iota((remote, remote), 0), iota((remote, remote), 1)
    first_row = total(jnp.where(low < high, sizes_column, 0), 0)
    first_column = total(jnp.where(high < low, sizes_row, 0), 1)
    before = total(jnp.where(iota((count, remote), 1) < column, sizes_row, 0), 1)
    rank = total(((column == row) & (across < down)).astype(jnp.int32), 1)
    place = jnp.where(column >= 0, before + rank, -1)
    seat = iota((count, width), 1)
    entry = total(jnp.where(place == seat, iota((count, width), 0) - count, 0), 0) + count
    halves = lax.shift_right_logical(first_column, 1)
    keep = 1 - total((halves == iota((remote, width), 1)).astype(jnp.int32), 0)
    plan[0:1, :] = entry
    plan[1:2, :] = keep
    last = jnp.maximum(lax.shift_right_logical(first_row + sizes_row, 1) - 1, 0)
    plan[2:3, 0:remote] = last


def kernel(
    sizes,
    ids_far,
    group_far,
    loop_far,
    features_ref,
    initial_ref,
    history_ref,
    weight_ref,
    values_ref,
    refreshed_ref,
    mail_ref,
    hist,
    feat,
    start,
    wgt,
    vals,
    turned,
    sources,
    outbox,
    fresh,
    outgoing,
    mixture,
    running,
    letters,
    plan_rows,
    plan,
    load_sem,
    tile_sem,
    store_sem,
    send_sem,
    recv_sem,
    mail_send,
    mail_recv,
    own_sem,
    plan_sem,
    ids_ref,
    group_ref,
    loop_ref,
    table_sem,
):
    group, loop, tiles, entries, edge, hidden, pairs = sizes
    remote = group + loop
    group_pos = lax.axis_index("grp")
    loop_pos = lax.axis_index("blk")

    loads = [
        pltpu.make_async_copy(history_ref, hist, load_sem.at[0]),
        pltpu.make_async_copy(features_ref, feat, load_sem.at[1]),
        pltpu.make_async_copy(values_ref, vals.at[pl.ds(0, tiles * entries)], load_sem.at[2]),
        pltpu.make_async_copy(initial_ref, start, load_sem.at[3]),
        pltpu.make_async_copy(weight_ref, wgt, load_sem.at[4]),
    ]
    tables = [
        pltpu.make_async_copy(group_far, group_ref, table_sem.at[0]),
        pltpu.make_async_copy(loop_far, loop_ref, table_sem.at[1]),
        pltpu.make_async_copy(ids_far, ids_ref, table_sem.at[2]),
    ]
    for load in tables + loads:
        load.start()

    peers = partners(group_pos, group, "grp") + partners(loop_pos, loop, "blk")

    barrier = pltpu.get_barrier_semaphore()
    for axis, there in peers:
        pl.semaphore_signal(barrier, inc=1, device_id={axis: there}, device_id_type=MESH)

    for load in tables:
        load.wait()
    loads[0].wait()
    for n, (axis, there) in enumerate(peers):
        block = group_ref[group_pos, there] if axis == "grp" else loop_ref[loop_pos, there]
        outbox[n] = hist[block]
    pl.semaphore_wait(barrier, len(peers))
    sends = []
    for n, (axis, there) in enumerate(peers):
        mine = tiles + group_pos if axis == "grp" else tiles + group + loop_pos
        copy = pltpu.make_async_remote_copy(
            src_ref=outbox.at[n],
            dst_ref=sources.at[mine],
            send_sem=send_sem.at[n],
            recv_sem=recv_sem.at[n],
            device_id={axis: there},
            device_id_type=MESH,
        )
        copy.start()
        sends.append(copy)
    sources[tiles + group_pos] = hist[group_ref[group_pos, group_pos]]
    sources[tiles + group + loop_pos] = hist[loop_ref[loop_pos, loop_pos]]
    loads[1].wait()
    sources[pl.ds(0, tiles)] = feat[...].astype(jnp.bfloat16)

    slot_plan(ids_ref, plan_rows, tiles, entries, remote, pairs)
    ordered = pltpu.make_async_copy(plan_rows, plan, plan_sem)
    ordered.start()
    vals[tiles * entries] = jnp.zeros((edge, edge), jnp.bfloat16)
    loads[2].wait()
    ordered.wait()

    def turn(m, _):
        both = jnp.concatenate([vals[plan[0, 2 * m]], vals[plan[0, 2 * m + 1]]], axis=0)
        turned[m] = both.T
        return 0

    lax.fori_loop(0, pairs, turn, 0, unroll=4)
    loads[3].wait()
    loads[4].wait()
    for copy in sends:
        copy.wait_recv()

    def gather(t, _):
        left = jnp.concatenate([vals[t * entries + k] for k in range(entries)], axis=1)
        right = jnp.concatenate([sources[ids_ref[t, k]] for k in range(entries)], axis=0)
        gathered = jnp.dot(left, right, preferred_element_type=jnp.float32)
        mixture[t] = (
            (1.0 - teleport) * gathered + teleport * start[t].astype(jnp.float32)
        ).astype(jnp.bfloat16)
        return 0

    lax.fori_loop(0, tiles, gather, 0, unroll=GATHER_UNROLL)

    def refresh(t, _):
        mixed = mixture[t]
        product = jnp.dot(mixed, wgt[...], preferred_element_type=jnp.float32)
        value = jnp.maximum(
            (1.0 - mapping_share) * mixed.astype(jnp.float32) + mapping_share * product, 0.0
        )
        fresh[t] = value
        outgoing[t] = value.astype(jnp.bfloat16)
        return 0

    lax.fori_loop(0, tiles, refresh, 0, unroll=REFRESH_UNROLL)
    store = pltpu.make_async_copy(fresh, refreshed_ref, store_sem)
    store.start()

    def gather_message(m, total):
        one = jnp.minimum(lax.div(plan[0, 2 * m], entries), tiles - 1)
        two = jnp.minimum(lax.div(plan[0, 2 * m + 1], entries), tiles - 1)
        right = jnp.concatenate([outgoing[one], outgoing[two]], axis=0)
        part = jnp.dot(turned[m], right, preferred_element_type=jnp.float32)
        total = jnp.where(plan[1, m] > 0, total, 0.0) + part
        running[m] = total.astype(jnp.bfloat16)
        return total

    lax.fori_loop(
        0, pairs, gather_message, jnp.zeros((edge, hidden), jnp.float32), unroll=MESSAGE_UNROLL
    )

    for n, (axis, there) in enumerate(peers):
        slot = there if axis == "grp" else group + there
        letters[n] = running[plan[2, slot]]
    letters[len(peers)] = running[plan[2, group_pos]]
    letters[len(peers) + 1] = running[plan[2, group + loop_pos]]
    mails = []
    for n, (axis, there) in enumerate(peers):
        mine = group_pos if axis == "grp" else group + loop_pos
        copy = pltpu.make_async_remote_copy(
            src_ref=letters.at[n],
            dst_ref=mail_ref.at[mine],
            send_sem=mail_send.at[n],
            recv_sem=mail_recv.at[n],
            device_id={axis: there},
            device_id_type=MESH,
        )
        copy.start()
        mails.append(copy)
    own = [
        pltpu.make_async_copy(letters.at[len(peers)], mail_ref.at[group_pos], own_sem.at[0]),
        pltpu.make_async_copy(
            letters.at[len(peers) + 1], mail_ref.at[group + loop_pos], own_sem.at[1]
        ),
    ]
    for copy in own:
        copy.start()
    for copy in sends:
        copy.wait_send()
    for copy in own:
        copy.wait()
    store.wait()
    for copy in mails:
        copy.wait()


def deliver(
    sizes, group_far, loop_far, fresh_ref, mail_ref, refreshed_ref, inbox_ref, sums, out_sem,
    group_ref, loop_ref, table_sem,
):
    group, loop, tiles = sizes
    group_pos = lax.axis_index("grp")
    loop_pos = lax.axis_index("blk")
    tables = [
        pltpu.make_async_copy(group_far, group_ref, table_sem.at[0]),
        pltpu.make_async_copy(loop_far, loop_ref, table_sem.at[1]),
    ]
    for load in tables:
        load.start()
    put_fresh = pltpu.make_async_copy(fresh_ref, refreshed_ref, out_sem.at[1])
    put_fresh.start()
    sums[...] = jnp.zeros_like(sums)
    for load in tables:
        load.wait()
    for n in range(group + loop):
        block = group_ref[group_pos, n] if n < group else loop_ref[loop_pos, n - group]
        sums[block] = sums[block] + mail_ref[n].astype(jnp.float32)
    put_sums = pltpu.make_async_copy(sums, inbox_ref, out_sem.at[0])
    put_sums.start()
    put_sums.wait()
    put_fresh.wait()


def body(features, initial, history, weight, column_ids, block_values, group_table, loop_table):
    group = lax.axis_size("grp")
    loop = lax.axis_size("blk")
    tiles, entries = column_ids.shape
    edge = block_values.shape[2]
    hidden = features.shape[1]
    remote = group + loop
    count = tiles * entries
    pairs = (count - tiles + remote) // 2
    pairs = -(-pairs // MESSAGE_UNROLL) * MESSAGE_UNROLL
    peers = remote - 2
    width = -(-2 * pairs // 128) * 128
    bf16, f32 = jnp.bfloat16, jnp.float32
    smem = pl.BlockSpec(memory_space=pltpu.SMEM)
    far = pl.BlockSpec(memory_space=pltpu.HBM)
    hbm = pl.BlockSpec(memory_space=pl.ANY)
    block = (tiles, edge, hidden)
    dma = pltpu.SemaphoreType.DMA
    refreshed, mail = pl.pallas_call(
        functools.partial(kernel, (group, loop, tiles, entries, edge, hidden, pairs)),
        out_shape=(
            jax.ShapeDtypeStruct(block, f32),
            jax.ShapeDtypeStruct((remote, edge, hidden), bf16),
        ),
        in_specs=[far] * 8,
        out_specs=(hbm, hbm),
        scratch_shapes=[
            pltpu.VMEM(block, bf16),
            pltpu.VMEM(block, f32),
            pltpu.VMEM(block, bf16),
            pltpu.VMEM((hidden, hidden), bf16),
            pltpu.VMEM((count + 1, edge, edge), bf16),
            pltpu.VMEM((pairs, edge, 2 * edge), bf16),
            pltpu.VMEM((tiles + remote, edge, hidden), bf16),
            pltpu.VMEM((peers, edge, hidden), bf16),
            pltpu.VMEM(block, f32),
            pltpu.VMEM(block, bf16),
            pltpu.VMEM(block, bf16),
            pltpu.VMEM((pairs, edge, hidden), bf16),
            pltpu.VMEM((remote, edge, hidden), bf16),
            pltpu.VMEM((8, width), jnp.int32),
            pltpu.SMEM((8, width), jnp.int32),
            dma((5,)),
            dma((1,)),
            dma,
            dma((peers,)),
            dma((peers,)),
            dma((peers,)),
            dma((peers,)),
            dma((2,)),
            dma,
            pltpu.SMEM((tiles, entries), jnp.int32),
            pltpu.SMEM((group, group), jnp.int32),
            pltpu.SMEM((loop, loop), jnp.int32),
            dma((3,)),
        ],
        compiler_params=pltpu.CompilerParams(
            collective_id=0, has_side_effects=True, vmem_limit_bytes=MAIN_LIMIT
        ),
    )(
        *[
            pltpu.with_memory_space_constraint(x, pltpu.HBM)
            for x in (
                column_ids,
                group_table[0],
                loop_table[0],
                features.reshape(block),
                initial.reshape(block),
                history.reshape(block),
                weight,
                block_values.reshape(count, edge, edge),
            )
        ],
    )
    refreshed, inbox = pl.pallas_call(
        functools.partial(deliver, (group, loop, tiles)),
        out_shape=(jax.ShapeDtypeStruct(block, f32), jax.ShapeDtypeStruct(block, f32)),
        in_specs=[far] * 2 + [pl.BlockSpec(memory_space=pltpu.VMEM)] * 2,
        out_specs=(hbm, hbm),
        scratch_shapes=[
            pltpu.VMEM(block, f32),
            dma((2,)),
            pltpu.SMEM((group, group), jnp.int32),
            pltpu.SMEM((loop, loop), jnp.int32),
            dma((2,)),
        ],
        compiler_params=pltpu.CompilerParams(vmem_limit_bytes=DELIVER_LIMIT),
    )(
        pltpu.with_memory_space_constraint(group_table[0], pltpu.HBM),
        pltpu.with_memory_space_constraint(loop_table[0], pltpu.HBM),
        refreshed,
        mail,
    )
    return (refreshed.reshape(tiles * edge, hidden), inbox.reshape(tiles * edge, hidden))


def solution(mesh):
    in_specs = (
        P(("blk", "grp"), None),
        P(("blk", "grp"), None),
        P(("blk", "grp"), None),
        P(),
        P(("blk", "grp"), None),
        P(("blk", "grp"), None, None, None),
        P("blk", None, None),
        P("grp", None, None),
    )
    out_specs = (P(("blk", "grp"), None), P(("blk", "grp"), None))
    return jax.shard_map(body, mesh=mesh, in_specs=in_specs, out_specs=out_specs, check_vma=False)
```

profile of v0, /device:TPU:0, one launch (start us, length us, event | category | flops | bytes accessed | tf_op | source)
XLA Modules:
  0.0 36.6 jit_solution(14132904522734457991)
XLA Ops:
  0.6 33.9 %shard_map.95 = (f32[12,128,256]{2,1,0:T(8,128)S(1)}, bf16[12,128,256]{2,1,0:T(8,128)(2,1)S(1)}) custom-call(s32[12,16]{1,0:T(8,128)} %ids_far.1, s32[8,8]{1,0:T(8,128)} %bitcast.12, s32[4,4]{1,0:T(4,128)} %bitcast.14, f32[12,128,256]{2,1,0:T(8,128)} %bitcast.9, bf16[12,128,256]{2,1,0:T(8,128)(2,1)} %bitcast.10, bf16[12,128,256]{2,1,0:T(8,128)(2,1)} %bitcast.11, ...), custom_call_target="tpu_custom_call" | custom-call | tf_op jit(solution)/shard_map/pallas_call | solution.py:295
  34.5 2.1 %shard_map.96 = (f32[12,128,256]{2,1,0:T(8,128)}, f32[12,128,256]{2,1,0:T(8,128)}) custom-call(s32[8,8]{1,0:T(8,128)} %bitcast.13, s32[4,4]{1,0:T(4,128)} %bitcast.15, f32[12,128,256]{2,1,0:T(8,128)S(1)} %get-tuple-element.6.fresh_ref, bf16[12,128,256]{2,1,0:T(8,128)(2,1)S(1)} %get-tuple-element.7.mail_ref), custom_call_target="tpu_custom_call" | custom-call | tf_op jit(solution)/shard_map/pallas_call | solution.py:351
where the time goes:
time: 36.8 us; the launch traced here: 36.6 us
  Pallas kernels  36 us (98%)
  between operations  0.64 us (2%)
    pallas_call x1, Pallas kernels, body(): pl.pallas_call(functools.partial(kernel, (group, loop, tiles, entries, ed...  33.9 us
    pallas_call x1, Pallas kernels, body(): pl.pallas_call(functools.partial(deliver, (group, loop, tiles)), out_shap...  2.08 us

commit v1 on v0

--- a/solution.py
+++ b/solution.py
@@ -15,22 +15,31 @@
 GATHER_UNROLL = 12
 REFRESH_UNROLL = 12
 MESSAGE_UNROLL = 32
-
-
-def partners(position, size, axis):
+LEAD = 0
+
+PULL_FAR = False
+MAIL_FAR = True
+
+
+def row_of(size):
+    row = 1
+    while size % (2 * row) == 0 and 4 * row * row <= size:
+        row *= 2
+    return row
+
+
+def along(position, size, far):
+    row = row_of(size)
+    lines = size // row
+    line, spot = lax.div(position, row), lax.rem(position, row)
     found = []
-    for step in range(size - 1, 0, -1):
-        if size & (size - 1) == 0:
-            there = position
-            bit = 1
-            while bit < size:
-                if step & bit:
-                    there = there + bit * (1 - 2 * lax.rem(lax.div(position, bit), 2))
-                bit *= 2
-            found.append((axis, there))
-        else:
-            found.append((axis, lax.rem(position + step, size)))
-    return found
+    for n in range(1, lines):
+        up = lines - n if far else line + n
+        down = line + n - lines if far else lines - 1 - n
+        there = jnp.where(line + n < lines, up, down)
+        found += [there * row + lax.rem(spot + j, row) for j in range(row)]
+    beside = [line * row + lax.rem(spot + j, row) for j in range(1, row)]
+    return found + beside if far else beside + found
 
 
 def slot_plan(ids_ref, plan, tiles, entries, remote, pairs):
@@ -104,6 +113,7 @@
     group_ref,
     loop_ref,
     table_sem,
+    go_sem,
 ):
     group, loop, tiles, entries, edge, hidden, pairs = sizes
     remote = group + loop
@@ -122,37 +132,54 @@
         pltpu.make_async_copy(loop_far, loop_ref, table_sem.at[1]),
         pltpu.make_async_copy(ids_far, ids_ref, table_sem.at[2]),
     ]
-    for load in tables + loads:
+    for load in tables + loads[:1]:
         load.start()
 
-    peers = partners(group_pos, group, "grp") + partners(loop_pos, loop, "blk")
+    everyone = [("grp", n) for n in along(group_pos, group, PULL_FAR)]
+    everyone += [("blk", lax.rem(loop_pos + n, loop)) for n in range(1, loop)]
+    posts = [("grp", n) for n in along(group_pos, group, MAIL_FAR)] + everyone[group - 1 :]
+    slot_of = lambda axis, there: there if axis == "grp" else group + there
+    mine_of = lambda axis: group_pos if axis == "grp" else group + loop_pos
 
     barrier = pltpu.get_barrier_semaphore()
-    for axis, there in peers:
+    for axis, there in everyone:
         pl.semaphore_signal(barrier, inc=1, device_id={axis: there}, device_id_type=MESH)
 
     for load in tables:
         load.wait()
     loads[0].wait()
-    for n, (axis, there) in enumerate(peers):
-        block = group_ref[group_pos, there] if axis == "grp" else loop_ref[loop_pos, there]
-        outbox[n] = hist[block]
-    pl.semaphore_wait(barrier, len(peers))
-    sends = []
-    for n, (axis, there) in enumerate(peers):
-        mine = tiles + group_pos if axis == "grp" else tiles + group + loop_pos
-        copy = pltpu.make_async_remote_copy(
-            src_ref=outbox.at[n],
-            dst_ref=sources.at[mine],
-            send_sem=send_sem.at[n],
-            recv_sem=recv_sem.at[n],
+    for load in loads[1:]:
+        load.start()
+    for n in range(remote):
+        outbox[n] = hist[group_ref[group_pos, n] if n < group else loop_ref[loop_pos, n - group]]
+    pl.semaphore_wait(barrier, len(everyone))
+
+    def pull(axis, there, arriving):
+        slot, mine = slot_of(axis, there), mine_of(axis)
+        return pltpu.make_async_remote_copy(
+            src_ref=outbox.at[slot],
+            dst_ref=sources.at[tiles + (slot if arriving else mine)],
+            send_sem=send_sem.at[slot],
+            recv_sem=recv_sem.at[slot if arriving else mine],
             device_id={axis: there},
             device_id_type=MESH,
         )
-        copy.start()
-        sends.append(copy)
-    sources[tiles + group_pos] = hist[group_ref[group_pos, group_pos]]
-    sources[tiles + group + loop_pos] = hist[loop_ref[loop_pos, loop_pos]]
+
+    for axis, there in everyone[group - 1 :]:
+        pull(axis, there, False).start()
+
+    def pull_group():
+        for axis, there in everyone[: group - 1]:
+            pull(axis, there, False).start()
+
+    leads = lax.rem(loop_pos, 2) == LEAD
+    takes_turns = loop % 2 == 0
+    if takes_turns:
+        pl.when(leads)(pull_group)
+    else:
+        pull_group()
+    sources[tiles + group_pos] = outbox[group_pos]
+    sources[tiles + group + loop_pos] = outbox[group + loop_pos]
     loads[1].wait()
     sources[pl.ds(0, tiles)] = feat[...].astype(jnp.bfloat16)
 
@@ -171,8 +198,30 @@
     lax.fori_loop(0, pairs, turn, 0, unroll=4)
     loads[3].wait()
     loads[4].wait()
-    for copy in sends:
-        copy.wait_recv()
+    beside = loop_pos + 1 - 2 * lax.rem(loop_pos, 2)
+    early = 3 * group // 8
+
+    def hand_over():
+        for axis, there in everyone[: group - 1 - early]:
+            pull(axis, there, True).wait_send()
+        pl.semaphore_signal(go_sem, inc=1, device_id={"blk": beside}, device_id_type=MESH)
+        for axis, there in everyone[group - 1 - early : group - 1]:
+            pull(axis, there, True).wait_send()
+
+    if takes_turns:
+
+        @pl.when(jnp.logical_not(leads))
+        def _():
+            pl.semaphore_wait(go_sem, 1)
+            pull_group()
+
+        hand_over()
+    else:
+        for axis, there in everyone[: group - 1]:
+            pull(axis, there, True).wait_send()
+
+    for axis, there in everyone:
+        pull(axis, there, True).wait_recv()
 
     def gather(t, _):
         left = jnp.concatenate([vals[t * entries + k] for k in range(entries)], axis=1)
@@ -212,39 +261,41 @@
         0, pairs, gather_message, jnp.zeros((edge, hidden), jnp.float32), unroll=MESSAGE_UNROLL
     )
 
-    for n, (axis, there) in enumerate(peers):
-        slot = there if axis == "grp" else group + there
-        letters[n] = running[plan[2, slot]]
-    letters[len(peers)] = running[plan[2, group_pos]]
-    letters[len(peers) + 1] = running[plan[2, group + loop_pos]]
-    mails = []
-    for n, (axis, there) in enumerate(peers):
-        mine = group_pos if axis == "grp" else group + loop_pos
-        copy = pltpu.make_async_remote_copy(
-            src_ref=letters.at[n],
-            dst_ref=mail_ref.at[mine],
-            send_sem=mail_send.at[n],
-            recv_sem=mail_recv.at[n],
+    def mail(axis, there, arriving):
+        slot, mine = slot_of(axis, there), mine_of(axis)
+        return pltpu.make_async_remote_copy(
+            src_ref=letters.at[slot],
+            dst_ref=mail_ref.at[slot if arriving else mine],
+            send_sem=mail_send.at[slot],
+            recv_sem=mail_recv.at[slot if arriving else mine],
             device_id={axis: there},
             device_id_type=MESH,
         )
-        copy.start()
-        mails.append(copy)
+
+    for slot in range(remote):
+        letters[slot] = running[plan[2, slot]]
+    if takes_turns:
+
+        @pl.when(leads)
+        def _():
+            pl.semaphore_wait(go_sem, 1)
+
+    for axis, there in posts:
+        mail(axis, there, False).start()
     own = [
-        pltpu.make_async_copy(letters.at[len(peers)], mail_ref.at[group_pos], own_sem.at[0]),
-        pltpu.make_async_copy(
-            letters.at[len(peers) + 1], mail_ref.at[group + loop_pos], own_sem.at[1]
-        ),
+        pltpu.make_async_copy(letters.at[slot], mail_ref.at[slot], own_sem.at[n])
+        for n, slot in enumerate((group_pos, group + loop_pos))
     ]
     for copy in own:
         copy.start()
-    for copy in sends:
-        copy.wait_send()
+    for axis, there in everyone[group - 1 :]:
+        pull(axis, there, True).wait_send()
+
     for copy in own:
         copy.wait()
     store.wait()
-    for copy in mails:
-        copy.wait()
+    for axis, there in everyone:
+        mail(axis, there, True).wait()
 
 
 def deliver(
@@ -284,7 +335,6 @@
     count = tiles * entries
     pairs = (count - tiles + remote) // 2
     pairs = -(-pairs // MESSAGE_UNROLL) * MESSAGE_UNROLL
-    peers = remote - 2
     width = -(-2 * pairs // 128) * 128
     bf16, f32 = jnp.bfloat16, jnp.float32
     smem = pl.BlockSpec(memory_space=pltpu.SMEM)
@@ -308,7 +358,7 @@
             pltpu.VMEM((count + 1, edge, edge), bf16),
             pltpu.VMEM((pairs, edge, 2 * edge), bf16),
             pltpu.VMEM((tiles + remote, edge, hidden), bf16),
-            pltpu.VMEM((peers, edge, hidden), bf16),
+            pltpu.VMEM((remote, edge, hidden), bf16),
             pltpu.VMEM(block, f32),
             pltpu.VMEM(block, bf16),
             pltpu.VMEM(block, bf16),
@@ -319,16 +369,17 @@
             dma((5,)),
             dma((1,)),
             dma,
-            dma((peers,)),
-            dma((peers,)),
-            dma((peers,)),
-            dma((peers,)),
+            dma((remote,)),
+            dma((remote,)),
+            dma((remote,)),
+            dma((remote,)),
             dma((2,)),
             dma,
             pltpu.SMEM((tiles, entries), jnp.int32),
             pltpu.SMEM((group, group), jnp.int32),
             pltpu.SMEM((loop, loop), jnp.int32),
             dma((3,)),
+            pltpu.SemaphoreType.REGULAR,
         ],
         compiler_params=pltpu.CompilerParams(
             collective_id=0, has_side_effects=True, vmem_limit_bytes=MAIN_LIMIT

time: 36.8 us -> 33.8 us (0.918)
  the two profiles are of different devices: /device:TPU:0 before, /device:TPU:9 now
where the time goes in v1:
time: 33.8 us; the launch traced here: 33.6 us
  Pallas kernels  32.9 us (97%)
  between operations  0.64 us (2%)
    pallas_call x1, Pallas kernels, body(): pl.pallas_call(functools.partial(kernel, (group, loop, tiles, entries, ed...  30.9 us
    pallas_call x1, Pallas kernels, body(): pl.pallas_call(functools.partial(deliver, (group, loop, tiles)), out_shap...  2.08 us

profile of v1, /device:TPU:9, one launch (start us, length us, event | category | flops | bytes accessed | tf_op | source)
XLA Modules:
  0.0 33.6 jit_solution(11666938165291444574)
XLA Ops:
  0.6 30.9 %shard_map.95 = (f32[12,128,256]{2,1,0:T(8,128)S(1)}, bf16[12,128,256]{2,1,0:T(8,128)(2,1)S(1)}) custom-call(s32[12,16]{1,0:T(8,128)} %ids_far.1, s32[8,8]{1,0:T(8,128)} %bitcast.12, s32[4,4]{1,0:T(4,128)} %bitcast.14, f32[12,128,256]{2,1,0:T(8,128)} %bitcast.9, bf16[12,128,256]{2,1,0:T(8,128)(2,1)} %bitcast.10, bf16[12,128,256]{2,1,0:T(8,128)(2,1)} %bitcast.11, ...), custom_call_target="tpu_custom_call" | custom-call | tf_op jit(solution)/shard_map/pallas_call | solution.py:345
  31.5 2.1 %shard_map.96 = (f32[12,128,256]{2,1,0:T(8,128)}, f32[12,128,256]{2,1,0:T(8,128)}) custom-call(s32[8,8]{1,0:T(8,128)} %bitcast.13, s32[4,4]{1,0:T(4,128)} %bitcast.15, f32[12,128,256]{2,1,0:T(8,128)S(1)} %get-tuple-element.6.fresh_ref, bf16[12,128,256]{2,1,0:T(8,128)(2,1)S(1)} %get-tuple-element.7.mail_ref), custom_call_target="tpu_custom_call" | custom-call | tf_op jit(solution)/shard_map/pallas_call | solution.py:402

commit v2 on v1

--- a/solution.py
+++ b/solution.py
@@ -14,11 +14,11 @@
 MESH = pl.DeviceIdType.MESH
 GATHER_UNROLL = 12
 REFRESH_UNROLL = 12
-MESSAGE_UNROLL = 32
-LEAD = 0
-
-PULL_FAR = False
-MAIL_FAR = True
+LEAD = 1
+EARLY = 3
+PULL = "near"
+LEAD_MAIL = "far"
+FOLLOW_MAIL = "far"
 
 
 def row_of(size):
@@ -28,18 +28,25 @@
     return row
 
 
-def along(position, size, far):
+def along(position, size, order):
     row = row_of(size)
     lines = size // row
     line, spot = lax.div(position, row), lax.rem(position, row)
+    last = lines - 1 - line
     found = []
     for n in range(1, lines):
-        up = lines - n if far else line + n
-        down = line + n - lines if far else lines - 1 - n
-        there = jnp.where(line + n < lines, up, down)
+        k = n - last
+        if order == "near":
+            up, down = line + n, line - k
+        elif order == "far":
+            up, down = lines - n, k - 1
+        else:
+            up = lines - 1 if n == 1 else line + n - 1
+            down = jnp.where(k == 1, 0, line + 1 - k)
+        there = jnp.where(n <= last, up, down)
         found += [there * row + lax.rem(spot + j, row) for j in range(row)]
     beside = [line * row + lax.rem(spot + j, row) for j in range(1, row)]
-    return found + beside if far else beside + found
+    return beside + found if order == "near" else found + beside
 
 
 def slot_plan(ids_ref, plan, tiles, entries, remote, pairs):
@@ -135,9 +142,12 @@
     for load in tables + loads[:1]:
         load.start()
 
-    everyone = [("grp", n) for n in along(group_pos, group, PULL_FAR)]
+    everyone = [("grp", n) for n in along(group_pos, group, PULL)]
     everyone += [("blk", lax.rem(loop_pos + n, loop)) for n in range(1, loop)]
-    posts = [("grp", n) for n in along(group_pos, group, MAIL_FAR)] + everyone[group - 1 :]
+    posts = [
+        [("grp", n) for n in along(group_pos, group, order)] + everyone[group - 1 :]
+        for order in (LEAD_MAIL, FOLLOW_MAIL)
+    ]
     slot_of = lambda axis, there: there if axis == "grp" else group + there
     mine_of = lambda axis: group_pos if axis == "grp" else group + loop_pos
 
@@ -199,9 +209,8 @@
     loads[3].wait()
     loads[4].wait()
     beside = loop_pos + 1 - 2 * lax.rem(loop_pos, 2)
-    early = 3 * group // 8
-
-    def hand_over():
+
+    def hand_over(early):
         for axis, there in everyone[: group - 1 - early]:
             pull(axis, there, True).wait_send()
         pl.semaphore_signal(go_sem, inc=1, device_id={"blk": beside}, device_id_type=MESH)
@@ -209,13 +218,14 @@
             pull(axis, there, True).wait_send()
 
     if takes_turns:
-
-        @pl.when(jnp.logical_not(leads))
+        follows = jnp.logical_not(leads)
+
+        @pl.when(follows)
         def _():
             pl.semaphore_wait(go_sem, 1)
             pull_group()
 
-        hand_over()
+        hand_over(EARLY * group // 8)
     else:
         for axis, there in everyone[: group - 1]:
             pull(axis, there, True).wait_send()
@@ -258,7 +268,7 @@
         return total
 
     lax.fori_loop(
-        0, pairs, gather_message, jnp.zeros((edge, hidden), jnp.float32), unroll=MESSAGE_UNROLL
+        0, pairs, gather_message, jnp.zeros((edge, hidden), jnp.float32), unroll=pairs
     )
 
     def mail(axis, there, arriving):
@@ -274,14 +284,17 @@
 
     for slot in range(remote):
         letters[slot] = running[plan[2, slot]]
+    def post(which):
+        if which == 0 and takes_turns:
+            pl.semaphore_wait(go_sem, 1)
+        for axis, there in posts[which]:
+            mail(axis, there, False).start()
+
     if takes_turns:
-
-        @pl.when(leads)
-        def _():
-            pl.semaphore_wait(go_sem, 1)
-
-    for axis, there in posts:
-        mail(axis, there, False).start()
+        pl.when(leads)(lambda: post(0))
+        pl.when(follows)(lambda: post(1))
+    else:
+        post(0)
     own = [
         pltpu.make_async_copy(letters.at[slot], mail_ref.at[slot], own_sem.at[n])
         for n, slot in enumerate((group_pos, group + loop_pos))
@@ -333,8 +346,7 @@
     hidden = features.shape[1]
     remote = group + loop
     count = tiles * entries
-    pairs = (count - tiles + remote) // 2
-    pairs = -(-pairs // MESSAGE_UNROLL) * MESSAGE_UNROLL
+    pairs = -(-(count - tiles + remote) // 8) * 4
     width = -(-2 * pairs // 128) * 128
     bf16, f32 = jnp.bfloat16, jnp.float32
     smem = pl.BlockSpec(memory_space=pltpu.SMEM)

time: 33.8 us -> 33.2 us (0.982)
  the two profiles are of different devices: /device:TPU:9 before, /device:TPU:0 now
where the time goes in v2:
time: 33.2 us; the launch traced here: 33 us
  Pallas kernels  32.4 us (98%)
  between operations  0.64 us (2%)
    pallas_call x1, Pallas kernels, body(): pl.pallas_call(functools.partial(kernel, (group, loop, tiles, entries, ed...  30.3 us
    pallas_call x1, Pallas kernels, body(): pl.pallas_call(functools.partial(deliver, (group, loop, tiles)), out_shap...  2.08 us

profile of v2, /device:TPU:0, one launch (start us, length us, event | category | flops | bytes accessed | tf_op | source)
XLA Modules:
  0.0 33.0 jit_solution(14230713233500317050)
XLA Ops:
  0.6 30.3 %shard_map.95 = (f32[12,128,256]{2,1,0:T(8,128)S(1)}, bf16[12,128,256]{2,1,0:T(8,128)(2,1)S(1)}) custom-call(s32[12,16]{1,0:T(8,128)} %ids_far.1, s32[8,8]{1,0:T(8,128)} %bitcast.12, s32[4,4]{1,0:T(4,128)} %bitcast.14, f32[12,128,256]{2,1,0:T(8,128)} %bitcast.9, bf16[12,128,256]{2,1,0:T(8,128)(2,1)} %bitcast.10, bf16[12,128,256]{2,1,0:T(8,128)(2,1)} %bitcast.11, ...), custom_call_target="tpu_custom_call" | custom-call | tf_op jit(solution)/shard_map/pallas_call | solution.py:357
  30.9 2.1 %shard_map.96 = (f32[12,128,256]{2,1,0:T(8,128)}, f32[12,128,256]{2,1,0:T(8,128)}) custom-call(s32[8,8]{1,0:T(8,128)} %bitcast.13, s32[4,4]{1,0:T(4,128)} %bitcast.15, f32[12,128,256]{2,1,0:T(8,128)S(1)} %get-tuple-element.6.fresh_ref, bf16[12,128,256]{2,1,0:T(8,128)(2,1)S(1)} %get-tuple-element.7.mail_ref), custom_call_target="tpu_custom_call" | custom-call | tf_op jit(solution)/shard_map/pallas_call | solution.py:414

commit v3 on v2

--- a/solution.py
+++ b/solution.py
@@ -92,6 +92,7 @@
     values_ref,
     refreshed_ref,
     mail_ref,
+    where_ref,
     hist,
     feat,
     start,
@@ -194,6 +195,12 @@
     sources[pl.ds(0, tiles)] = feat[...].astype(jnp.bfloat16)
 
     slot_plan(ids_ref, plan_rows, tiles, entries, remote, pairs)
+    lane = lax.broadcasted_iota(jnp.int32, where_ref.shape, 1)
+    where = jnp.zeros(where_ref.shape, jnp.int32)
+    for n in range(remote):
+        block = group_ref[group_pos, n] if n < group else loop_ref[loop_pos, n - group]
+        where = jnp.where(lane == n, block, where)
+    where_ref[...] = where
     ordered = pltpu.make_async_copy(plan_rows, plan, plan_sem)
     ordered.start()
     vals[tiles * entries] = jnp.zeros((edge, edge), jnp.bfloat16)
@@ -311,26 +318,15 @@
         mail(axis, there, True).wait()
 
 
-def deliver(
-    sizes, group_far, loop_far, fresh_ref, mail_ref, refreshed_ref, inbox_ref, sums, out_sem,
-    group_ref, loop_ref, table_sem,
-):
-    group, loop, tiles = sizes
-    group_pos = lax.axis_index("grp")
-    loop_pos = lax.axis_index("blk")
-    tables = [
-        pltpu.make_async_copy(group_far, group_ref, table_sem.at[0]),
-        pltpu.make_async_copy(loop_far, loop_ref, table_sem.at[1]),
-    ]
-    for load in tables:
-        load.start()
+def deliver(sizes, where_ref, fresh_ref, mail_ref, refreshed_ref, inbox_ref, sums, out_sem):
+    remote = sizes
     put_fresh = pltpu.make_async_copy(fresh_ref, refreshed_ref, out_sem.at[1])
     put_fresh.start()
+    row = where_ref[0:1, :]
+    lane = lax.broadcasted_iota(jnp.int32, row.shape, 1)
+    blocks = [jnp.sum(jnp.where(lane == n, row, 0)) for n in range(remote)]
     sums[...] = jnp.zeros_like(sums)
-    for load in tables:
-        load.wait()
-    for n in range(group + loop):
-        block = group_ref[group_pos, n] if n < group else loop_ref[loop_pos, n - group]
+    for n, block in enumerate(blocks):
         sums[block] = sums[block] + mail_ref[n].astype(jnp.float32)
     put_sums = pltpu.make_async_copy(sums, inbox_ref, out_sem.at[0])
     put_sums.start()
@@ -354,14 +350,15 @@
     hbm = pl.BlockSpec(memory_space=pl.ANY)
     block = (tiles, edge, hidden)
     dma = pltpu.SemaphoreType.DMA
-    refreshed, mail = pl.pallas_call(
+    refreshed, mail, where = pl.pallas_call(
         functools.partial(kernel, (group, loop, tiles, entries, edge, hidden, pairs)),
         out_shape=(
             jax.ShapeDtypeStruct(block, f32),
             jax.ShapeDtypeStruct((remote, edge, hidden), bf16),
+            jax.ShapeDtypeStruct((8, -(-remote // 128) * 128), jnp.int32),
         ),
         in_specs=[far] * 8,
-        out_specs=(hbm, hbm),
+        out_specs=(hbm, hbm, pl.BlockSpec(memory_space=pltpu.VMEM)),
         scratch_shapes=[
             pltpu.VMEM(block, bf16),
             pltpu.VMEM(block, f32),
@@ -412,24 +409,13 @@
         ],
     )
     refreshed, inbox = pl.pallas_call(
-        functools.partial(deliver, (group, loop, tiles)),
+        functools.partial(deliver, remote),
         out_shape=(jax.ShapeDtypeStruct(block, f32), jax.ShapeDtypeStruct(block, f32)),
-        in_specs=[far] * 2 + [pl.BlockSpec(memory_space=pltpu.VMEM)] * 2,
+        in_specs=[pl.BlockSpec(memory_space=pltpu.VMEM)] * 3,
         out_specs=(hbm, hbm),
-        scratch_shapes=[
-            pltpu.VMEM(block, f32),
-            dma((2,)),
-            pltpu.SMEM((group, group), jnp.int32),
-            pltpu.SMEM((loop, loop), jnp.int32),
-            dma((2,)),
-        ],
+        scratch_shapes=[pltpu.VMEM(block, f32), dma((2,))],
         compiler_params=pltpu.CompilerParams(vmem_limit_bytes=DELIVER_LIMIT),
-    )(
-        pltpu.with_memory_space_constraint(group_table[0], pltpu.HBM),
-        pltpu.with_memory_space_constraint(loop_table[0], pltpu.HBM),
-        refreshed,
-        mail,
-    )
+    )(where, refreshed, mail)
     return (refreshed.reshape(tiles * edge, hidden), inbox.reshape(tiles * edge, hidden))
 
 

time: 33.2 us -> 32.8 us (0.988)
  Pallas kernels: 32.4 us -> 32 us
    pallas_call x1, Pallas kernels: 2.08 us -> 1.68 us  [body(): pl.pallas_call(functools.partial(deliver, remote), out_shape=(jax.ShapeDt...]
where the time goes in v3:
time: 32.8 us; the launch traced here: 32.6 us
  Pallas kernels  32 us (98%)
  between operations  0.64 us (2%)
    pallas_call x1, Pallas kernels, body(): pl.pallas_call(functools.partial(kernel, (group, loop, tiles, entries, ed...  30.3 us
    pallas_call x1, Pallas kernels, body(): pl.pallas_call(functools.partial(deliver, remote), out_shape=(jax.ShapeDt...  1.68 us

profile of v3, /device:TPU:0, one launch (start us, length us, event | category | flops | bytes accessed | tf_op | source)
XLA Modules:
  0.0 32.6 jit_solution(4229098637876066794)
XLA Ops:
  0.6 30.3 %shard_map.95 = (f32[12,128,256]{2,1,0:T(8,128)S(1)}, bf16[12,128,256]{2,1,0:T(8,128)(2,1)S(1)}, s32[8,128]{1,0:T(8,128)S(1)}) custom-call(s32[12,16]{1,0:T(8,128)} %ids_far.1, s32[8,8]{1,0:T(8,128)} %bitcast.12, s32[4,4]{1,0:T(4,128)} %bitcast.13, f32[12,128,256]{2,1,0:T(8,128)} %bitcast.9, bf16[12,128,256]{2,1,0:T(8,128)(2,1)} %bitcast.10, ...), custom_call_target="tpu_custom_call" | custom-call | tf_op jit(solution)/shard_map/pallas_call | solution.py:353
  30.9 1.7 %shard_map.96 = (f32[12,128,256]{2,1,0:T(8,128)}, f32[12,128,256]{2,1,0:T(8,128)}) custom-call(s32[8,128]{1,0:T(8,128)S(1)} %get-tuple-element.7.where_ref, f32[12,128,256]{2,1,0:T(8,128)S(1)} %get-tuple-element.8.fresh_ref, bf16[12,128,256]{2,1,0:T(8,128)(2,1)S(1)} %get-tuple-element.9.mail_ref), custom_call_target="tpu_custom_call" | custom-call | tf_op jit(solution)/shard_map/pallas_call | solution.py:411
